TPU v7x, 32 devices: a whole 2x2x4 slice. The times are simulated.
32 devices in a mesh: dp: 8 (over z, x), expert: 4 (over y, core).
Axes of the slice: x: 2, y: 2, z: 4, core: 2. Of those that a mesh axis runs over, the one named last changes fastest.
Arguments:
- queries: bfloat16 [256, 2048], P(('dp', 'expert')), may hold values from -8 to 8
- fresh_key: bfloat16 [256, 256], P(('dp', 'expert')), may hold values from -4 to 4
- fresh_value: bfloat16 [256, 256], P(('dp', 'expert')), may hold values from -4 to 4
- cached_keys: bfloat16 [256, 128, 256], P(('dp', 'expert')), may hold values from -8 to 8
- cached_values: bfloat16 [256, 128, 256], P(('dp', 'expert')), may hold values from -4 to 4
- lengths: int32 [256], P(('dp', 'expert')), may hold values from 2 to 128
- sink_logit_rows: float32 [32], replicated, may hold values from 1 to 5
- residual: bfloat16 [256, 2880], P('dp', 'expert'), may hold values from -6 to 6
- o_weight: bfloat16 [2880, 2048], P('expert'), may hold values from -0.125 to 0.125
- norm_gain: float32 [2880], replicated, may hold values from 0.5 to 1.5
- expert_ids: int32 [256, 4], replicated, may hold values from 0 to 7, all different within a row; in each aligned block of 32 rows (0 to 31, 32 to 63, ...) at most 32 rows name the same one
- route_weights: float32 [256, 4], replicated, may hold values from 0.1 to 0.6
- w_gate_up: bfloat16 [8, 2, 2880, 2880], P('dp', None, 'expert'), may hold values from -0.109375 to 0.109375
- w_down: bfloat16 [8, 2880, 2880], P('dp', 'expert'), may hold values from -0.15625 to 0.15625
Outputs:
- layer_out: bfloat16 [256, 2880], P('dp', 'expert')
Inputs may be any that keep to these rules, and one draw needn't show every extreme that they name: `expert_ids`: each row names 4 different experts; among any aligned block of 32 rows no expert is named by more than 32 rows.
All inputs are finite; a program needn't handle non-finite values.
Results may differ from a plain program's by a relative error of at most 0.018.
Values may be sent and summed in bfloat16 or wider, within the bound.
No kernel may reach another device: no remote copies, remote signals or barrier semaphores. Data moves between devices by JAX's collectives and lax.ppermute only.
A program may use at most 64 MiB of HBM per device.

v0:
```python
import math
import jax
import jax.numpy as jnp
from jax import lax
from jax.sharding import PartitionSpec as P

D = 2880
QUERY_HEADS = 32
KEY_VALUE_HEADS = 4
HEAD_SIZE = 64
WINDOW_LENGTH = 128
TOP = 4
norm_eps = 1e-05
swish_alpha = 1.702


def attend(queries, fresh_key, fresh_value, cached_keys, cached_values, lengths, sink_logit_rows):
    batch_count = queries.shape[0]
    head_groups = QUERY_HEADS // KEY_VALUE_HEADS
    query_head_rows = queries.reshape(batch_count, KEY_VALUE_HEADS, head_groups, HEAD_SIZE)
    key_rows = cached_keys.reshape(batch_count, WINDOW_LENGTH, KEY_VALUE_HEADS, HEAD_SIZE)
    value_rows = cached_values.reshape(batch_count, WINDOW_LENGTH, KEY_VALUE_HEADS, HEAD_SIZE)
    score_scale = 1.0 / math.sqrt(HEAD_SIZE)
    cache_scores = (
        jnp.einsum("bkgd,bwkd->bkgw", query_head_rows, key_rows, preferred_element_type=jnp.float32)
        * score_scale
    )
    own_scores = (
        jnp.einsum(
            "npwm,npm->npw",
            query_head_rows,
            fresh_key.reshape(batch_count, KEY_VALUE_HEADS, HEAD_SIZE),
            preferred_element_type=jnp.float32,
        )
        * score_scale
    )
    slots = jnp.arange(WINDOW_LENGTH, dtype=jnp.int32)
    valid = (slots[None, :] >= (WINDOW_LENGTH - lengths)[:, None])[:, None, None, :]
    sink_terms = sink_logit_rows.reshape(KEY_VALUE_HEADS, head_groups)[None]
    masked = jnp.where(valid, cache_scores, -jnp.inf)
    top = jnp.maximum(jnp.maximum(jnp.max(masked, axis=-1), own_scores), sink_terms)
    cache_exp = jnp.where(valid, jnp.exp(masked - top[..., None]), 0.0)
    self_exp = jnp.exp(own_scores - top)
    total = jnp.sum(cache_exp, axis=-1) + self_exp + jnp.exp(sink_terms - top)
    cache_prob = (cache_exp / total[..., None]).astype(jnp.bfloat16)
    own_probability = (self_exp / total).astype(jnp.bfloat16)
    blended = jnp.einsum(
        "bkgw,bwkd->bkgd", cache_prob, value_rows, preferred_element_type=jnp.float32
    )
    blended = blended + own_probability.astype(jnp.float32)[..., None] * fresh_value.reshape(
        batch_count, KEY_VALUE_HEADS, 1, HEAD_SIZE
    ).astype(jnp.float32)
    return blended.reshape(batch_count, QUERY_HEADS * HEAD_SIZE).astype(jnp.bfloat16)


def slot_onehot(named, capacity):
    counts = jnp.cumsum(named.astype(jnp.int32), axis=1) - 1
    places = jnp.arange(capacity, dtype=jnp.int32)
    return named[:, None, :] & (counts[:, None, :] == places[None, :, None])


def receiver_slots(expert_ids, route_weights, expert, blocks, capacity):
    picked = expert_ids == expert
    named = jnp.any(picked, axis=1).reshape(blocks, -1)
    weight_at = jnp.sum(jnp.where(picked, route_weights, 0.0), axis=1).reshape(blocks, -1)
    onehot = slot_onehot(named, capacity)
    slot_weight = jnp.sum(jnp.where(onehot, weight_at[:, None, :], 0.0), axis=2)
    return (onehot, slot_weight)


def sender_slots(my_ids, experts, capacity):
    labels = jnp.arange(experts, dtype=jnp.int32)
    named = jnp.any(my_ids[None, :, :] == labels[:, None, None], axis=2)
    return slot_onehot(named, capacity)


def body(
    queries,
    fresh_key,
    fresh_value,
    cached_keys,
    cached_values,
    lengths,
    sink_logit_rows,
    residual,
    o_weight,
    norm_gain,
    expert_ids,
    route_weights,
    w_gate_up,
    w_down,
):
    attended = attend(
        queries, fresh_key, fresh_value, cached_keys, cached_values, lengths, sink_logit_rows
    )
    projected = lax.dot_general(
        lax.all_gather(attended, "expert", axis=0, tiled=True),
        o_weight,
        (((1,), (1,)), ((), ())),
        preferred_element_type=jnp.float32,
    )
    stream = (residual.astype(jnp.float32) + projected).astype(jnp.bfloat16)
    wide = stream.astype(jnp.float32)
    group_rows = stream.shape[0]
    columns = stream.shape[1]
    experts = lax.axis_size("dp")
    capacity = 2 * group_rows * TOP // experts
    gain_cols = lax.dynamic_slice_in_dim(norm_gain, lax.axis_index("expert") * columns, columns)
    squares = lax.psum(jnp.sum(wide * wide, axis=1), "expert")
    score_scale = lax.rsqrt(squares / D + norm_eps)
    outgoing = (wide * score_scale[:, None] * gain_cols[None, :]).astype(jnp.bfloat16)
    onehot_in, slot_weight = receiver_slots(
        expert_ids, route_weights, lax.axis_index("dp"), experts, capacity
    )
    my_ids = lax.dynamic_slice_in_dim(expert_ids, lax.axis_index("dp") * group_rows, group_rows, 0)
    onehot_out = sender_slots(my_ids, experts, capacity)
    outbound = jnp.einsum(
        "ect,td->ecd", onehot_out.astype(jnp.bfloat16), outgoing, preferred_element_type=jnp.float32
    ).astype(jnp.bfloat16)
    received = lax.all_to_all(outbound, "dp", split_axis=0, concat_axis=0, tiled=True)
    rows = received.reshape(experts * capacity, columns)
    gate_up = w_gate_up[0]
    down = w_down[0]
    both = jnp.einsum(
        "rc,hfc->rhf",
        lax.all_gather(rows, "expert", axis=1, tiled=True),
        gate_up,
        preferred_element_type=jnp.float32,
    )
    gate = both[:, 0]
    up = both[:, 1]
    hidden = ((up + 1.0) * gate * jax.nn.sigmoid(swish_alpha * gate)).astype(jnp.bfloat16)
    summed = lax.psum_scatter(
        lax.dot_general(
            down, hidden, (((0,), (1,)), ((), ())), preferred_element_type=jnp.float32
        ).astype(jnp.bfloat16),
        "expert",
        scatter_dimension=0,
        tiled=True,
    ).astype(jnp.float32)
    contribution = (summed * slot_weight.reshape(1, -1)).astype(jnp.bfloat16)
    contribution = contribution.T.reshape(experts, capacity, columns)
    returned = lax.all_to_all(contribution, "dp", split_axis=0, concat_axis=0, tiled=True)
    returned_sum = jnp.einsum(
        "ect,ecd->td",
        onehot_out.astype(jnp.float32),
        returned.astype(jnp.float32),
        precision=lax.Precision.HIGHEST,
    )
    return (wide + returned_sum).astype(jnp.bfloat16)


def solution(mesh):
    placed = (
        P(("dp", "expert"), None),
        P(("dp", "expert"), None),
        P(("dp", "expert"), None),
        P(("dp", "expert"), None, None),
        P(("dp", "expert"), None, None),
        P(("dp", "expert")),
        P(),
        P("dp", "expert"),
        P("expert", None),
        P(),
        P(),
        P(),
        P("dp", None, "expert", None),
        P("dp", "expert", None),
    )
    return jax.shard_map(
        body, mesh=mesh, in_specs=placed, out_specs=P("dp", "expert"), check_vma=False
    )
```

profile of v0, /device:TPU:0, one launch (start us, length us, event | category | flops | bytes accessed | tf_op | source)
XLA Modules:
  0.0 138.2 jit_solution(12964307490870638373)
XLA Ops:
  6.5 0.8 broadcast_subtract_fusion
  7.4 0.9 reshape.81
  8.4 1.3 copy.27
  9.7 1.4 reshape.94
  11.1 0.7 max.14
  11.8 0.9 fusion.48
  14.3 1.3 copy.28
  15.6 0.7 reshape.87
  16.3 1.4 %fusion.12 = bf16[8,4,8,64]{3,2,1,0:T(8,128)(2,1)S(1)} fusion(bf16[8,128,4,64]{1,3,2,0:T(8,128)(2,1)S(1)} %bitcast.48, f32[8,4,8,128]{3,2,1,0:T(8,128)} %copy-done.1, f32[8,4,64]{2,1,0:T(4,128)} %reshape.87, f32[8,4,8]{2,1,0:T(4,128)} %get-tuple-element.7, f32[8,4,8]{2,1,0:T(4,128)} %get-tuple-element.8, f32[8,4,8]{2,1,0:T(4,128)S(1)} %maximum_maximum_fusion, ...), kind=kOutput, calls=%fused_computation.11 | convolution fusion | flops 4374528 | bytes 700416 | tf_op jit(solution)/shard_map/bkgw,bwkd->bkgd/dot_general | solution.py:47
  17.8 6.5 %all_gather.6 = bf16[32,2048]{1,0:T(8,128)(2,1)S(1)} all-gather(bf16[8,2048]{1,0:T(8,128)(2,1)S(1)} %convert_element_type.86), channel_id=1, replica_groups=mesh['dp'=8,'expert'=4] {'expert'}, dimensions={0}, use_global_device_ids=true | all-gather | bytes 163840 | tf_op jit(solution)/shard_map/all_gather | solution.py:97
  24.4 1.9 %multiply_reduce_fusion = (f32[32]{0:T(128)S(1)}, f32[32,720]{1,0:T(8,128)S(1)}) fusion(bf16[32,2048]{1,0:T(8,128)(2,1)S(1)} %all_gather.6, bf16[720,2048]{1,0:T(8,128)(2,1)S(1)} %copy-done, bf16[32,720]{1,0:T(8,128)(2,1)} %param.21), kind=kOutput, calls=%fused_computation.35 | convolution fusion | flops 94510048 | bytes 3218560 | tf_op jit(solution)/shard_map/dot_general | solution.py:96
  26.2 7.5 %psum.7 = f32[32]{0:T(128)S(1)} all-reduce(f32[32]{0:T(128)S(1)} %get-tuple-element.11), channel_id=1, replica_groups=mesh['dp'=8,'expert'=4] {'expert'}, use_global_device_ids=true, to_apply=%region_5.6 | all-reduce | flops 32 | bytes 256 | tf_op jit(solution)/shard_map/psum | solution.py:109
  33.7 0.8 constant_dynamic-slice_fusion
  34.7 0.8 dynamic_slice.7
  35.8 16.2 %all_to_all.10 = bf16[8,32,720]{2,1,0:T(8,128)(2,1)S(1)} all-to-all(bf16[8,32,720]{2,1,0:T(8,128)(2,1)S(1)} %convolution_convert_fusion), channel_id=1, replica_groups=mesh['dp'=8,'expert'=4] {'dp'}, dimensions={0} | all-to-all | bytes 737280 | tf_op jit(solution)/shard_map/all_to_all | solution.py:120
  52.1 0.9 copy.30
  53.1 17.9 %all-gather.2.cloned.1.call-done = bf16[256,2880]{0,1:T(8,128)(2,1)} async-done(((bf16[256,720]{0,1:T(8,128)(2,1)}), bf16[256,2880]{0,1:T(8,128)(2,1)}) %all-gather.2.cloned.1.call-update) | async-done | bytes 1474576 | tf_op jit(solution)/shard_map/all_gather | solution.py:126
  71.0 6.3 %fusion = f32[256,2,720]{0,2,1:T(8,128)S(1)} fusion(bf16[1,2,720,2880]{3,2,1,0:T(8,128)(2,1)} %param.26, bf16[256,2880]{0,1:T(8,128)(2,1)} %all-gather.2.cloned.1.call-done), kind=kOutput, calls=%fused_computation | convolution fusion | flops 2123366400 | bytes 11243520 | tf_op jit(solution)/shard_map/rc,hfc->rhf/dot_general | solution.py:124
  77.3 5.3 %fusion.7 = bf16[2880,256]{1,0:T(8,128)(2,1)} fusion(bf16[1,720,2880]{2,1,0:T(8,128)(2,1)} %param.27, f32[256,2,720]{0,2,1:T(8,128)S(1)} %fusion), kind=kOutput, calls=%fused_computation.5 | convolution fusion | flops 1063895040 | bytes 7096320 | tf_op jit(solution)/shard_map/dot_general | solution.py:134
  83.2 27.0 %reduce-scatter.2.cloned.1.call-done = bf16[720,256]{1,0:T(8,128)(2,1)} async-done(((bf16[2880,256]{1,0:T(8,128)(2,1)}), bf16[720,256]{1,0:T(8,128)(2,1)}) %reduce-scatter.2.cloned.1.call-update) | async-done | bytes 368656 | tf_op jit(solution)/shard_map/reduce_scatter | solution.py:133
  110.2 1.8 %fusion.20 = bf16[256,720]{0,1:T(8,128)(2,1)} fusion(bf16[720,256]{1,0:T(8,128)(2,1)} %reduce-scatter.2.cloned.1.call-done, f32[256]{0:T(256)S(1)} %mul.93), kind=kLoop, calls=%fused_computation.23 | loop fusion | flops 552960 | bytes 738304 | tf_op jit(solution)/shard_map/transpose | solution.py:142
  112.0 1.2 copy.31
  113.2 17.2 %all_to_all.11 = bf16[8,32,720]{2,1,0:T(8,128)(2,1)S(1)} all-to-all(bf16[8,32,720]{2,1,0:T(8,128)(2,1)S(1)} %bitcast.47), channel_id=1, replica_groups=mesh['dp'=8,'expert'=4] {'dp'}, dimensions={0} | all-to-all | bytes 737280 | tf_op jit(solution)/shard_map/all_to_all | solution.py:143
  130.4 1.0 fusion.16
  (37 shorter events, 3.1 us)
Async XLA Ops:
  6.5 17.8 %copy-start = (bf16[720,2048]{1,0:T(8,128)(2,1)S(1)}, bf16[720,2048]{1,0:T(8,128)(2,1)}, u32[]{:S(2)}) copy-start(bf16[720,2048]{1,0:T(8,128)(2,1)} %param.22) | copy-start | bytes 8847364
  6.5 9.1 %copy-start.4 = (bf16[8,256]{1,0:T(8,128)(2,1)S(1)}, bf16[8,256]{1,0:T(8,128)(2,1)}, u32[]{:S(2)}) copy-start(bf16[8,256]{1,0:T(8,128)(2,1)} %param.16) | copy-start | bytes 12292
  6.5 64.4 %all-gather.2.cloned.1.call-start = ((), (), s32[]{:S(2)}) async-start(), calls=%async_computation.3 | async-start | bytes 1843200 | tf_op jit(solution)/shard_map/all_gather | solution.py:126
  7.4 8.9 %copy-start.3 = (pred[8,128]{1,0:T(8,128)(4,1)}, pred[8,128]{1,0:T(8,128)(4,1)S(1)}, u32[]{:S(2)}) copy-start(pred[8,128]{1,0:T(8,128)(4,1)S(1)} %iota_compare_fusion.3) | copy-start | bytes 3076
  13.0 0.6 copy-start.1
  53.0 57.2 %reduce-scatter.2.cloned.1.call-start = ((), (), s32[]{:S(2)}) async-start(), calls=%async_computation.4 | async-start | bytes 1843200 | tf_op jit(solution)/shard_map/reduce_scatter | solution.py:133
  77.3 5.3 %copy-start.2 = (s32[256,4]{0,1:T(4,128)S(1)}, s32[256,4]{0,1:T(4,128)}, u32[]{:S(2)}) copy-start(s32[256,4]{0,1:T(4,128)} %param.24) | copy-start | bytes 12292
  77.3 5.6 %copy-start.5 = (f32[256,4]{0,1:T(4,128)S(1)}, f32[256,4]{0,1:T(4,128)}, u32[]{:S(2)}) copy-start(f32[256,4]{0,1:T(4,128)} %param.25) | copy-start | bytes 12292
Sparse Core Ops, SparseCore 0:
  53.1 17.7 all-gather.1
  82.7 27.4 reduce-scatter.1
where the time goes:
time: 139 us; the launch traced here: 138 us
  blocking collectives  47.5 us (34%)
  waiting for transfers between devices  44.9 us (32%)
  matrix products  17.4 us (13%)
  between operations  13.5 us (10%)
  local copies, waits for them, and re-layouts  10.8 us (8%)
  other arithmetic  4.1 us (3%)
    reduce_scatter x1, waiting for transfers between devices, body(): lax.psum_scatter(lax.dot_general(down, hidden, (((0,), (1,)), ((), ())),...  27 us
    all_gather x1, waiting for transfers between devices, body(): lax.all_gather(rows, 'expert', axis=1, tiled=True)  17.9 us
    all_to_all x1, blocking collectives, body(): lax.all_to_all(contribution, 'dp', split_axis=0, concat_axis=0, tiled=True)  17.2 us
    all_to_all x1, blocking collectives, body(): lax.all_to_all(outbound, 'dp', split_axis=0, concat_axis=0, tiled=True)  16.2 us
    psum x1, blocking collectives, body(): squares = lax.psum(jnp.sum(wide * wide, axis=1), 'expert')  7.47 us
    all_gather x1, blocking collectives, body(): lax.all_gather(attended, 'expert', axis=0, tiled=True)  6.54 us
    dot_general x1, matrix products, body(): jnp.einsum('rc,hfc->rhf', lax.all_gather(rows, 'expert', axis=1, tiled=Tr...  6.32 us
    dot_general x1, matrix products, body(): lax.dot_general(down, hidden, (((0,), (1,)), ((), ())), preferred_element...  5.28 us
  transfers between devices with their start and end apart: 2, of which 2 were waited for; matrix products, arithmetic and copies ran while one was open for 0% of the time, Pallas kernels for 0%

commit v1 on v0

--- a/solution.py
+++ b/solution.py
@@ -12,6 +12,18 @@
 TOP = 4
 norm_eps = 1e-05
 swish_alpha = 1.702
+
+
+def ring_product(x, axis, dim, term):
+    size, mine = (lax.axis_size(axis), lax.axis_index(axis))
+    backward = [(i, (i - 1) % size) for i in range(size)]
+    extent = x.shape[dim]
+    block = x
+    running = term(block, mine * extent)
+    for hop in range(1, size):
+        block = lax.ppermute(block, axis, backward)
+        running = running + term(block, (mine + hop) % size * extent)
+    return running
 
 
 def attend(queries, fresh_key, fresh_value, cached_keys, cached_values, lengths, sink_logit_rows):
@@ -121,11 +133,16 @@
     rows = received.reshape(experts * capacity, columns)
     gate_up = w_gate_up[0]
     down = w_down[0]
-    both = jnp.einsum(
-        "rc,hfc->rhf",
-        lax.all_gather(rows, "expert", axis=1, tiled=True),
-        gate_up,
-        preferred_element_type=jnp.float32,
+    both = ring_product(
+        rows,
+        "expert",
+        1,
+        lambda shard, start: jnp.einsum(
+            "rc,hfc->rhf",
+            shard,
+            lax.dynamic_slice_in_dim(gate_up, start, shard.shape[1], axis=2),
+            preferred_element_type=jnp.float32,
+        ),
     )
     gate = both[:, 0]
     up = both[:, 1]

time: 139 us -> 133 us (0.957)
  waiting for transfers between devices: 44.9 us -> 33.9 us
  starting transfers between devices: 0.04 us -> 3.82 us
  matrix products: 17.4 us -> 20.5 us
    all_gather x1 -> x0, waiting for transfers between devices: 17.9 us -> none  [body(): lax.all_gather(rows, 'expert', axis=1, tiled=True)]
    ppermute x0 -> x3, waiting for transfers between devices: none -> 7.97 us  [ring_product(): block = lax.ppermute(block, axis, backward)]
    dot_general x1 -> x4, matrix products: 6.32 us -> 11.5 us  [body(): jnp.einsum('rc,hfc->rhf', shard, lax.dynamic_slice_in_dim(gate_up, start,...]
    ppermute x0 -> x3, starting transfers between devices: none -> 3.82 us  [ring_product(): block = lax.ppermute(block, axis, backward)]
    dot_general x1, matrix products: 5.28 us -> 3.15 us  [body(): lax.dot_general(down, hidden, (((0,), (1,)), ((), ())), preferred_element...]
    unnamed x14 -> x16, local copies, waits for them, and re-layouts: 3.05 us -> 3.54 us
  transfers between devices with their start and end apart: 2 -> 4, of which waited for: 2 -> 3; matrix products, arithmetic and copies ran while one was open for 0% -> 7% of each run, Pallas kernels for 0% -> 0%
where the time goes in v1:
time: 133 us
  blocking collectives  47.5 us (36%)
  waiting for transfers between devices  33.9 us (25%)
  matrix products  20.5 us (15%)
  between operations  13.6 us (10%)
  local copies, waits for them, and re-layouts  9.87 us (7%)
  starting transfers between devices  3.82 us (3%)
  other arithmetic  3.35 us (3%)
    reduce_scatter x1, waiting for transfers between devices, body(): lax.psum_scatter(lax.dot_general(down, hidden, (((0,), (1,)), ((), ())),...  25.9 us
    all_to_all x1, blocking collectives, body(): lax.all_to_all(contribution, 'dp', split_axis=0, concat_axis=0, tiled=True)  17.2 us
    all_to_all x1, blocking collectives, body(): lax.all_to_all(outbound, 'dp', split_axis=0, concat_axis=0, tiled=True)  16.2 us
    dot_general x4, matrix products, body(): jnp.einsum('rc,hfc->rhf', shard, lax.dynamic_slice_in_dim(gate_up, start,...  11.5 us
    ppermute x3, waiting for transfers between devices, ring_product(): block = lax.ppermute(block, axis, backward)  7.97 us
    psum x1, blocking collectives, body(): squares = lax.psum(jnp.sum(wide * wide, axis=1), 'expert')  7.48 us
    all_gather x1, blocking collectives, body(): lax.all_gather(attended, 'expert', axis=0, tiled=True)  6.54 us
    ppermute x3, starting transfers between devices, ring_product(): block = lax.ppermute(block, axis, backward)  3.82 us
  transfers between devices with their start and end apart: 4, of which 3 were waited for; matrix products, arithmetic and copies ran while one was open for 7% of the time, Pallas kernels for 0%

profile of v1, /device:TPU:0, one launch (start us, length us, event | category | flops | bytes accessed | tf_op | source)
XLA Modules:
  0.0 132.5 jit_solution(8633928777382676332)
XLA Ops:
  6.6 2.2 %copy.30 = bf16[8,128,256]{1,2,0:T(8,128)(2,1)} copy(bf16[8,128,256]{2,1,0:T(8,128)(2,1)} %param.18) | data formatting | bytes 1048576 | tf_op args[4]
  8.7 0.9 reshape.85
  9.6 1.3 copy.29
  11.7 1.4 %reshape.91 = f32[8,4,64]{2,1,0:T(4,128)} reshape(bf16[8,256]{1,0:T(8,128)(2,1)} %param.16) | data formatting | bytes 12288 | tf_op jit(solution)/shard_map/convert_element_type | solution.py:64
  15.3 1.5 %fusion.23 = bf16[8,4,8,64]{3,2,1,0:T(8,128)(2,1)S(1)} fusion(bf16[8,128,4,64]{1,3,2,0:T(8,128)(2,1)} %bitcast.69, f32[8,4,8,128]{3,2,1,0:T(8,128)S(1)} %get-tuple-element.10, f32[8,4,64]{2,1,0:T(4,128)} %reshape.91, f32[8,4,8]{2,1,0:T(4,128)S(1)} %get-tuple-element.7, f32[8,4,8]{2,1,0:T(4,128)S(1)} %get-tuple-element.8, ...), kind=kOutput, calls=%fused_computation.21 | convolution fusion | flops 4374528 | bytes 700416 | tf_op jit(solution)/shard_map/bkgw,bwkd->bkgd/dot_general | solution.py:59
  17.0 6.5 %all_gather.3 = bf16[32,2048]{1,0:T(8,128)(2,1)S(1)} all-gather(bf16[8,2048]{1,0:T(8,128)(2,1)S(1)} %convert_element_type.86), channel_id=1, replica_groups=mesh['dp'=8,'expert'=4] {'expert'}, dimensions={0}, use_global_device_ids=true | all-gather | bytes 163840 | tf_op jit(solution)/shard_map/all_gather | solution.py:109
  23.8 1.9 %multiply_reduce_fusion = (f32[32]{0:T(128)S(1)}, f32[32,720]{1,0:T(8,128)S(1)}) fusion(bf16[32,2048]{1,0:T(8,128)(2,1)S(1)} %all_gather.3, bf16[720,2048]{1,0:T(8,128)(2,1)S(1)} %copy-done, bf16[32,720]{1,0:T(8,128)(2,1)} %param.21), kind=kOutput, calls=%fused_computation.48 | convolution fusion | flops 94510048 | bytes 3218560 | tf_op jit(solution)/shard_map/dot_general | solution.py:108
  25.6 7.5 %psum.7 = f32[32]{0:T(128)S(1)} all-reduce(f32[32]{0:T(128)S(1)} %get-tuple-element.11), channel_id=1, replica_groups=mesh['dp'=8,'expert'=4] {'expert'}, use_global_device_ids=true, to_apply=%region_5.6 | all-reduce | flops 32 | bytes 256 | tf_op jit(solution)/shard_map/psum | solution.py:121
  34.3 16.2 %all_to_all.10 = bf16[8,32,720]{2,1,0:T(8,128)(2,1)S(1)} all-to-all(bf16[8,32,720]{2,1,0:T(8,128)(2,1)S(1)} %convolution_convert_fusion), channel_id=1, replica_groups=mesh['dp'=8,'expert'=4] {'dp'}, dimensions={0} | all-to-all | bytes 737280 | tf_op jit(solution)/shard_map/all_to_all | solution.py:132
  50.5 0.9 copy.33
  51.4 5.3 %collective-permute-done = bf16[256,720]{0,1:T(8,128)(2,1)} collective-permute-done((bf16[256,720]{0,1:T(8,128)(2,1)}, bf16[256,720]{0,1:T(8,128)(2,1)}, u32[]{:S(2)}, u32[]{:S(2)}) %collective-permute-start) | collective-permute-done | bytes 368672 | tf_op jit(solution)/shard_map/ppermute | solution.py:24
  56.8 1.9 %collective-permute-start.1 = (bf16[256,720]{0,1:T(8,128)(2,1)}, bf16[256,720]{0,1:T(8,128)(2,1)}, u32[]{:S(2)}, u32[]{:S(2)}) collective-permute-start(bf16[256,720]{0,1:T(8,128)(2,1)} %collective-permute-done), channel_id=1, source_target_pairs={{0,3},{1,0},{2,1},{3,2},{4,7},{5,4},{6,5},{7,6},{8,11},{9,8},{10,9... | collective-permute-start | bytes 1105928 | tf_op jit(solution)/shard_map/ppermute | solution.py:24
  58.7 2.7 %fusion.14 = f32[256,2,720]{0,2,1:T(8,128)S(1)} fusion(bf16[256,720,1]{1,0,2:T(8,128)(2,1)S(1)} %bitcast.66, bf16[1,2,720,2880]{3,2,1,0:T(8,128)(2,1)} %param.26, s32[]{:T(128)S(6)} %select_n.49), kind=kOutput, calls=%fused_computation.10 | convolution fusion | flops 530841600 | bytes 4055044 | tf_op jit(solution)/shard_map/rc,hfc->rhf/dot_general | solution.py:140
  61.4 2.6 %collective-permute-done.1 = bf16[256,720]{0,1:T(8,128)(2,1)} collective-permute-done((bf16[256,720]{0,1:T(8,128)(2,1)}, bf16[256,720]{0,1:T(8,128)(2,1)}, u32[]{:S(2)}, u32[]{:S(2)}) %collective-permute-start.1) | collective-permute-done | bytes 368672 | tf_op jit(solution)/shard_map/ppermute | solution.py:24
  64.0 1.9 %collective-permute-start.2 = (bf16[256,720]{0,1:T(8,128)(2,1)}, bf16[256,720]{0,1:T(8,128)(2,1)S(1)}, u32[]{:S(2)}, u32[]{:S(2)}) collective-permute-start(bf16[256,720]{0,1:T(8,128)(2,1)} %collective-permute-done.1), channel_id=1, source_target_pairs={{0,3},{1,0},{2,1},{3,2},{4,7},{5,4},{6,5},{7,6},{8,11},{9,8},{10,9... | collective-permute-start | bytes 1105928 | tf_op jit(solution)/shard_map/ppermute | solution.py:24
  66.0 2.9 %fusion.12 = f32[256,2,720]{0,2,1:T(8,128)S(1)} fusion(bf16[1,2,720,2880]{3,2,1,0:T(8,128)(2,1)} %param.26, s32[]{:T(128)S(6)} %select_n.51, bf16[256,720]{0,1:T(8,128)(2,1)} %collective-permute-done), kind=kOutput, calls=%fused_computation.8 | convolution fusion | flops 530841600 | bytes 4055044 | tf_op jit(solution)/shard_map/rc,hfc->rhf/dot_general | solution.py:140
  68.9 3.0 %fusion.10 = f32[256,2,720]{0,2,1:T(8,128)S(1)} fusion(bf16[1,2,720,2880]{3,2,1,0:T(8,128)(2,1)} %param.26, s32[]{:T(128)S(6)} %select_n.53, bf16[256,720]{0,1:T(8,128)(2,1)} %collective-permute-done.1), kind=kOutput, calls=%fused_computation.6 | convolution fusion | flops 530841600 | bytes 4055044 | tf_op jit(solution)/shard_map/rc,hfc->rhf/dot_general | solution.py:140
  71.9 2.8 %add_add_fusion = f32[256,2,720]{0,2,1:T(8,128)S(1)} fusion(f32[256,2,720]{0,2,1:T(8,128)S(1)} %fusion.10, f32[256,2,720]{0,2,1:T(8,128)S(1)} %fusion.14, f32[256,2,720]{0,2,1:T(8,128)S(1)} %fusion.12, bf16[1,2,720,2880]{3,2,1,0:T(8,128)(2,1)} %param.26, s32[]{:T(128)S(6)} %select_n.55, bf16[256,720]{0,1:T(8,128)(2,1)S(1)} %collective-permute-done.2), kind=kOutput, calls=%fused_computation.16 | convolution fusion | flops 531947520 | bytes 8478724 | tf_op jit(solution)/shard_map/rc,hfc->rhf/dot_general | solution.py:140
  74.8 3.2 %fusion.5 = bf16[2880,256]{1,0:T(8,128)(2,1)} fusion(bf16[1,720,2880]{2,1,0:T(8,128)(2,1)S(1)} %bitcast.73, f32[256,2,720]{0,2,1:T(8,128)S(1)} %add_add_fusion), kind=kOutput, calls=%fused_computation.3 | convolution fusion | flops 1063895040 | bytes 7096320 | tf_op jit(solution)/shard_map/dot_general | solution.py:151
  78.6 25.9 %reduce-scatter.2.cloned.1.call-done = bf16[720,256]{1,0:T(8,128)(2,1)} async-done(((bf16[2880,256]{1,0:T(8,128)(2,1)}), bf16[720,256]{1,0:T(8,128)(2,1)}) %reduce-scatter.2.cloned.1.call-update) | async-done | bytes 368656 | tf_op jit(solution)/shard_map/reduce_scatter | solution.py:150
  104.5 1.8 %fusion.31 = bf16[256,720]{0,1:T(8,128)(2,1)} fusion(bf16[720,256]{1,0:T(8,128)(2,1)} %reduce-scatter.2.cloned.1.call-done, f32[256]{0:T(256)S(1)} %mul.106), kind=kLoop, calls=%fused_computation.33 | loop fusion | flops 552960 | bytes 738304 | tf_op jit(solution)/shard_map/transpose | solution.py:159
  106.3 1.2 copy.34
  107.5 17.2 %all_to_all.11 = bf16[8,32,720]{2,1,0:T(8,128)(2,1)S(1)} all-to-all(bf16[8,32,720]{2,1,0:T(8,128)(2,1)S(1)} %bitcast.68), channel_id=1, replica_groups=mesh['dp'=8,'expert'=4] {'dp'}, dimensions={0} | all-to-all | bytes 737280 | tf_op jit(solution)/shard_map/all_to_all | solution.py:160
  124.7 1.0 fusion.27
  (46 shorter events, 5.2 us)
Async XLA Ops:
  6.5 17.3 %copy-start = (bf16[720,2048]{1,0:T(8,128)(2,1)S(1)}, bf16[720,2048]{1,0:T(8,128)(2,1)}, u32[]{:S(2)}) copy-start(bf16[720,2048]{1,0:T(8,128)(2,1)} %param.22) | copy-start | bytes 8847364
  6.5 6.5 %copy-start.2 = (bf16[8,256]{1,0:T(8,128)(2,1)S(1)}, bf16[8,256]{1,0:T(8,128)(2,1)}, u32[]{:S(2)}) copy-start(bf16[8,256]{1,0:T(8,128)(2,1)} %param.15) | copy-start | bytes 12292
  6.5 7.2 %copy-start.4 = (f32[32]{0:T(128)S(1)}, f32[32]{0:T(128)}, u32[]{:S(2)}) copy-start(f32[32]{0:T(128)} %param.20) | copy-start | bytes 388
  6.5 98.0 %reduce-scatter.2.cloned.1.call-start = ((), (), s32[]{:S(2)}) async-start(), calls=%async_computation.3 | async-start | bytes 1843200 | tf_op jit(solution)/shard_map/reduce_scatter | solution.py:150
  8.7 14.8 %copy-start.1 = (s32[256,4]{0,1:T(4,128)S(1)}, s32[256,4]{0,1:T(4,128)}, u32[]{:S(2)}) copy-start(s32[256,4]{0,1:T(4,128)} %param.24) | copy-start | bytes 12292
  51.4 5.4 %collective-permute-start = (bf16[256,720]{0,1:T(8,128)(2,1)}, bf16[256,720]{0,1:T(8,128)(2,1)}, u32[]{:S(2)}, u32[]{:S(2)}) collective-permute-start(bf16[256,720]{0,1:T(8,128)(2,1)} %copy.33), channel_id=1, source_target_pairs={{0,3},{1,0},{2,1},{3,2},{4,7},{5,4},{6,5},{7,6},{8,11},{9,8},{10,9... | collective-permute-start | bytes 1105928 | tf_op jit(solution)/shard_map/ppermute | solution.py:24
  56.8 7.3 %collective-permute-start.1 = (bf16[256,720]{0,1:T(8,128)(2,1)}, bf16[256,720]{0,1:T(8,128)(2,1)}, u32[]{:S(2)}, u32[]{:S(2)}) collective-permute-start(bf16[256,720]{0,1:T(8,128)(2,1)} %collective-permute-done), channel_id=1, source_target_pairs={{0,3},{1,0},{2,1},{3,2},{4,7},{5,4},{6,5},{7,6},{8,11},{9,8},{10,9... | collective-permute-start | bytes 1105928 | tf_op jit(solution)/shard_map/ppermute | solution.py:24
  64.0 7.8 %collective-permute-start.2 = (bf16[256,720]{0,1:T(8,128)(2,1)}, bf16[256,720]{0,1:T(8,128)(2,1)S(1)}, u32[]{:S(2)}, u32[]{:S(2)}) collective-permute-start(bf16[256,720]{0,1:T(8,128)(2,1)} %collective-permute-done.1), channel_id=1, source_target_pairs={{0,3},{1,0},{2,1},{3,2},{4,7},{5,4},{6,5},{7,6},{8,11},{9,8},{10,9... | collective-permute-start | bytes 1105928 | tf_op jit(solution)/shard_map/ppermute | solution.py:24
  68.8 5.9 %slice-start = ((s8[4239360]{0:T(1024)(128)(4,1)}), s8[4194304]{0:T(1024)(128)(4,1)S(1)}, s32[]{:S(2)}) async-start(s8[4239360]{0:T(1024)(128)(4,1)} %bitcast.72), calls=%async_computation.4 | async-start | bytes 8388608
  71.9 2.9 %slice-start.1 = ((s8[4239360]{0:T(1024)(128)(4,1)}), s8[45056]{0:T(1024)(128)(4,1)S(1)}, s32[]{:S(2)}) async-start(s8[4239360]{0:T(1024)(128)(4,1)} %bitcast.72), calls=%async_computation.5 | async-start | bytes 90112
  74.8 3.2 %copy-start.3 = (f32[256,4]{0,1:T(4,128)S(1)}, f32[256,4]{0,1:T(4,128)}, u32[]{:S(2)}) copy-start(f32[256,4]{0,1:T(4,128)} %param.25) | copy-start | bytes 12292
Sparse Core Ops, SparseCore 0:
  78.1 26.3 reduce-scatter.1
